TPU v7x, 32 devices: a whole 2x2x4 slice. The times are simulated.
32 devices in a mesh: blk: 16 (over z, x, core), pair: 2 (over y).
Axes of the slice: x: 2, y: 2, z: 4, core: 2. Of those that a mesh axis runs over, the one named last changes fastest.
Arguments:
- vertex: bfloat16 [16, 2048, 2048], P('blk', 'pair'), may hold values from -0.125 to 0.125
- left_phase: bfloat16 [16, 2048, 512], P('blk', 'pair'), may hold values from -6 to 6
- right_phase: bfloat16 [16, 2048, 512], P('blk'), may hold values from -6 to 6
- tiles: bfloat16 [64, 512, 512], P('blk'), may hold values from -0.25 to 0.25
- orders: int32 [16], P('blk'), may hold values from 512 to 2048, as said below
- momentum: int32 [512], replicated, may hold values from 0 to 63
- frequency: int32 [512], replicated, may hold values from 0 to 31
Outputs:
- suscept: bfloat16 [64, 512, 512], P('blk', 'pair')
- sigma: float32 [2048], P(('blk', 'pair'))
Inputs may be any that keep to these rules, and one draw needn't show every extreme that they name: `orders`: every order is at least 512 and at most 2048; some walker has order exactly 2048.
All inputs are finite; a program needn't handle non-finite values.
Results may differ from a plain program's by a relative error of at most 0.0075.
Values may be sent and summed in bfloat16 or wider, within the bound.
A program may use at most 64 MiB of HBM per device.

v0:
```python
import math

import jax
import jax.numpy as jnp
from jax import lax
from jax.experimental import pallas as pl
from jax.experimental.pallas import tpu as pltpu
from jax.sharding import PartitionSpec as P

NMOM = 64
NFREQ = 32
LANES = 128
CHUNKS = 4
SPLIT = 2
MESH = pl.DeviceIdType.MESH
OWN, PEER, ACROSS, RELAYED, FORWARDED = range(5)


def contract(a, b, dims, precision=None):
    return lax.dot_general(
        a, b, (dims, ((), ())), preferred_element_type=jnp.float32, precision=precision
    )


def body(sizes, order_ref, mom_ref, freq_ref, vertex_hbm, left_hbm, right_hbm, tiles_hbm,
         out_ref, sigma_ref,
         vertex, left, right, tiles, carried, partial, sending, arrived, greens, inner, acc,
         cells_ref, sig_send, sig_recv, load_sem, y_send, y_recv, x_send, x_recv, z_send, z_recv,
         p_send, p_recv, f_send, f_recv, s_send, s_recv,
         chi, o_sem):
    n_blk, n_pair, height, breadth, states, n_tiles = sizes
    count = n_blk * n_pair
    half = states // n_pair
    b = lax.axis_index("blk")
    p = lax.axis_index("pair")
    me = b * n_pair + p
    chip = b // 2
    core = lax.rem(b, 2)
    odd = lax.rem(chip, 2)
    step = 1 - 2 * odd
    across = (lax.rem(b + 2 * step + n_blk, n_blk), p)
    along = (lax.rem(b + 4 * step + n_blk, n_blk), p)
    peer = (b + 1 - 2 * core, p)
    other = (b, 1 - p)
    forwards_across = lax.rem(odd + core, 2) == 0

    barrier = pltpu.get_barrier_semaphore()

    def greet(i, carry):
        to = lax.rem(me + i, count)
        pl.semaphore_signal(barrier, inc=1, device_id=(to // n_pair, lax.rem(to, n_pair)),
                            device_id_type=MESH)
        return carry

    lax.fori_loop(1, count, greet, 0)

    pieces = 4
    block = height // pieces
    wide = states // SPLIT

    def load_right(h):
        cols = pl.ds(h * wide, wide)
        return pltpu.make_async_copy(right_hbm.at[0, :, cols], right.at[h], load_sem.at[h])

    load_right(0).start()
    load_vertex = []
    for i in range(pieces):
        rows = pl.ds(i * block, block)
        copy = pltpu.make_async_copy(vertex_hbm.at[0, rows], vertex.at[rows], load_sem.at[SPLIT + i])
        copy.start()
        load_vertex.append(copy)
    load_left = pltpu.make_async_copy(left_hbm.at[0], left, load_sem.at[SPLIT + pieces])
    load_left.start()
    for h in range(1, SPLIT):
        load_right(h).start()
    load_tiles = pltpu.make_async_copy(tiles_hbm, tiles, load_sem.at[SPLIT + 1 + pieces])
    load_tiles.start()

    order = order_ref[0]
    scale = 1.0 / math.sqrt(breadth)
    per_split = CHUNKS // SPLIT
    size = states // per_split
    per_half = half // size

    def chunk(which, k):
        index = lax.rem(which * per_half + k % per_split, per_split)
        return (pl.ds(pl.multiple_of(index * size, size), size),
                pl.ds(k // per_split * wide, wide))

    def exchange(k):
        rows = chunk(1 - p, k)
        return pltpu.make_async_remote_copy(
            src_ref=sending.at[*rows], dst_ref=arrived.at[*rows], send_sem=y_send.at[k],
            recv_sem=y_recv.at[k], device_id=other, device_id_type=MESH)

    def arrival(k):
        rows = chunk(p, k)
        return pltpu.make_async_remote_copy(
            src_ref=sending.at[*rows], dst_ref=arrived.at[*rows], send_sem=y_send.at[k],
            recv_sem=y_recv.at[k], device_id=other, device_id_type=MESH)

    def hop(source, target, k, send, recv, device):
        rows = chunk(p, k)
        return pltpu.make_async_remote_copy(
            src_ref=greens.at[source, *rows], dst_ref=greens.at[target, *rows], send_sem=send.at[k],
            recv_sem=recv.at[k], device_id=device, device_id_type=MESH)

    def to_across(k):
        return hop(OWN, ACROSS, k, x_send, x_recv, across)

    def to_peer(k):
        return hop(OWN, PEER, k, p_send, p_recv, peer)

    def to_along(k):
        return hop(ACROSS, RELAYED, k, z_send, z_recv, along)

    def forward(source, k):
        return hop(source, FORWARDED, k, f_send, f_recv, peer)

    for h in range(SPLIT):
        load_right(h).wait()

        def mask_right(i, carry):
            rows = pl.ds(pl.multiple_of(i * 256, 256), 256)
            ids = i * 256 + lax.broadcasted_iota(jnp.int32, (256, wide), 0)
            right[h, rows, :] = jnp.where(ids < order, right[h, rows, :], jnp.zeros((), jnp.bfloat16))
            return carry

        lax.fori_loop(0, breadth // 256, mask_right, 0)
        for i in range(pieces):
            rows = pl.ds(i * block, block)
            if h == 0:
                load_vertex[i].wait()
            product = contract(vertex[rows, :], right[h], ((1,), (0,)))
            ids = p * height + i * block + lax.broadcasted_iota(jnp.int32, (block, wide), 0)
            carried[rows, :] = jnp.where(ids < order, product, 0.0).astype(jnp.bfloat16)
        if h == 0:
            load_left.wait()
            pl.semaphore_wait(barrier, count - 1)
        cols = pl.ds(h * wide, wide)
        for part in range(n_pair):
            which = lax.rem(1 - p + part, n_pair)
            rows = pl.ds(pl.multiple_of(which * half, half), half)
            product = contract(left[:, rows], carried[...], ((0,), (0,))) * scale
            partial[rows, cols] = product
            sending[rows, cols] = product.astype(jnp.bfloat16)
            for k in range(per_half):
                exchange(h * per_split + part * per_half + k).start()

    ids_m = lax.broadcasted_iota(jnp.int32, (NMOM, half), 0)
    pick_mom = (ids_m == mom_ref[p]).astype(jnp.bfloat16)
    ids_f = lax.broadcasted_iota(jnp.int32, (LANES, states), 0)
    pick_freq = (ids_f == freq_ref[...]).astype(jnp.bfloat16)
    own_rows = pl.ds(pl.multiple_of(p * half, half), half)

    def compute_inner(slot, slot_index):
        upper = greens[slot, own_rows, :]
        total = jnp.zeros((half, states), jnp.float32)
        for t in range(n_tiles):
            value = contract(upper, tiles[t], ((1,), (0,))).astype(jnp.bfloat16)
            inner[slot_index, pl.ds(t * half, half), :] = value
            total = total + value.astype(jnp.float32)
        high = total.astype(jnp.bfloat16)
        low = (total - high.astype(jnp.float32)).astype(jnp.bfloat16)
        return contract(pick_mom, high, ((1,), (0,))) + contract(pick_mom, low, ((1,), (0,)))

    def compute_cells(slot, folded, first=False):
        picked = contract(pick_freq, greens[slot], ((1,), (0,)))
        value = contract(folded, picked, ((1,), (1,)), lax.Precision.HIGHEST)
        cells_ref[...] = value if first else cells_ref[...] + value

    out_scale = 1.0 / math.sqrt(states)

    def store(t):
        return pltpu.make_async_copy(chi.at[t], out_ref.at[t], o_sem.at[t])

    def compute_chi(slot, slot_index, first=False, last=False):
        for t in range(n_tiles):
            rows = pl.ds(t * half, half)
            value = contract(inner[slot_index, rows, :], greens[slot], ((1,), (1,)))
            if not first:
                value = acc[rows, :] + value
            if last:
                chi[t] = (value * out_scale).astype(jnp.bfloat16)
                store(t).start()
            else:
                acc[rows, :] = value

    def take_y(k):
        arrival(k).wait_recv()
        rows = chunk(p, k)
        greens[OWN, *rows] = (
            partial[*rows] + arrived[*rows].astype(jnp.float32)
        ).astype(jnp.bfloat16)
        to_across(k).start()
        to_peer(k).start()

    def take_x(k):
        to_across(k).wait_recv()
        to_along(k).start()

        @pl.when(forwards_across)
        def _():
            forward(ACROSS, k).start()

    def take_z(k):
        to_along(k).wait_recv()

        @pl.when(jnp.logical_not(forwards_across))
        def _():
            forward(RELAYED, k).start()

    folds = {}
    upper_last = CHUNKS - per_split + per_half - 1
    lag = 2
    for s in range(CHUNKS + 2 * lag):
        if s < CHUNKS:
            take_y(s)
        if 0 <= s - lag < CHUNKS:
            take_x(s - lag)
        if 0 <= s - 2 * lag < CHUNKS:
            take_z(s - 2 * lag)
        if s == upper_last:
            load_tiles.wait()
            folds[OWN] = compute_inner(OWN, 0)
        if s == CHUNKS - 1:
            compute_cells(OWN, folds[OWN], first=True)
            compute_chi(OWN, 0, first=True)
        if s == CHUNKS:
            for k in range(CHUNKS):
                to_peer(k).wait_recv()
            folds[PEER] = compute_inner(PEER, 1)
            folds[ACROSS] = compute_inner(ACROSS, 2)
        if s == CHUNKS + 1:
            compute_cells(PEER, folds[PEER])
            compute_cells(ACROSS, folds[ACROSS])
            compute_chi(PEER, 1)
        if s == CHUNKS + lag:
            folds[RELAYED] = compute_inner(RELAYED, 3)
            for k in range(upper_last + 1):
                forward(ACROSS, k).wait_recv()
            folds[FORWARDED] = compute_inner(FORWARDED, 4)

    compute_cells(RELAYED, folds[RELAYED])
    for k in range(upper_last + 1, CHUNKS):
        forward(ACROSS, k).wait_recv()
    compute_cells(FORWARDED, folds[FORWARDED])

    own_cells = NMOM * NFREQ // count
    cells = cells_ref[...]
    rows_d = lax.broadcasted_iota(jnp.int32, (count, NMOM), 0)
    cols_m = lax.broadcasted_iota(jnp.int32, (count, NMOM), 1)
    spread = jnp.zeros((count, LANES), jnp.float32)
    if own_cells >= NFREQ:
        group = own_cells // NFREQ
        for k in range(group):
            pick = (cols_m == rows_d * group + k).astype(jnp.float32)
            value = contract(pick, cells, ((1,), (0,)), lax.Precision.HIGHEST)
            spread = spread + (pltpu.roll(value, NFREQ * k, 1) if k else value)
    else:
        group = NFREQ // own_cells
        for k in range(group):
            pick = (rows_d == cols_m * group + k).astype(jnp.float32)
            value = contract(pick, cells, ((1,), (0,)), lax.Precision.HIGHEST)
            spread = spread + (pltpu.roll(value, LANES - own_cells * k, 1) if k else value)
    factor = 1.0 / math.sqrt(5.0 * n_tiles * n_blk * states * states / (NMOM * NFREQ))
    spread = spread * (factor * out_scale)
    sig_send[...] = spread.reshape(count, 1, LANES)

    def owner(i):
        to = lax.rem(me + i, count)
        return pltpu.make_async_remote_copy(
            src_ref=sig_send.at[to], dst_ref=sig_recv.at[i - 1], send_sem=s_send.at[i - 1],
            recv_sem=s_recv.at[i - 1], device_id=(to // n_pair, lax.rem(to, n_pair)),
            device_id_type=MESH)

    def send_cells(i, carry):
        owner(i).start()
        return carry

    lax.fori_loop(1, count, send_cells, 0)

    compute_chi(ACROSS, 2)
    compute_chi(RELAYED, 3)
    compute_chi(FORWARDED, 4, last=True)

    for k in range(CHUNKS):
        exchange(k).wait_send()
        to_across(k).wait_send()
        to_peer(k).wait_send()
        to_along(k).wait_send()
        forward(ACROSS, k).wait_send()

    for t in range(n_tiles):
        store(t).wait()

    def take_cells(i, carry):
        owner(i).wait()
        return carry

    lax.fori_loop(1, count, take_cells, 0)
    total = jnp.sum(sig_recv[...], axis=0) + sig_send[me]
    sigma_ref[...] = total[:, :own_cells]


def solution(mesh):
    n_blk, n_pair = mesh.shape["blk"], mesh.shape["pair"]
    count = n_blk * n_pair

    def per_device(vertex, left_phase, right_phase, tiles, orders, momentum, frequency):
        height, breadth = vertex.shape[1], vertex.shape[2]
        states = right_phase.shape[2]
        n_tiles = tiles.shape[0]
        half = states // n_pair
        sizes = (n_blk, n_pair, height, breadth, states, n_tiles)
        bf16, f32 = jnp.bfloat16, jnp.float32
        dma = pltpu.SemaphoreType.DMA
        chi, cells = pl.pallas_call(
            lambda *refs: body(sizes, *refs),
            out_shape=(
                jax.ShapeDtypeStruct((n_tiles, half, states), bf16),
                jax.ShapeDtypeStruct((1, NMOM * NFREQ // count), f32),
            ),
            in_specs=[
                pl.BlockSpec(memory_space=pltpu.SMEM),
                pl.BlockSpec(memory_space=pltpu.VMEM),
                pl.BlockSpec(memory_space=pltpu.VMEM),
            ] + [pl.BlockSpec(memory_space=pltpu.HBM)] * 4,
            out_specs=(
                pl.BlockSpec(memory_space=pltpu.HBM),
                pl.BlockSpec(memory_space=pltpu.VMEM),
            ),
            scratch_shapes=[
                pltpu.VMEM((height, breadth), bf16),
                pltpu.VMEM((height, states), bf16),
                pltpu.VMEM((SPLIT, breadth, states // SPLIT), bf16),
                pltpu.VMEM((n_tiles, states, states), bf16),
                pltpu.VMEM((height, states // SPLIT), bf16),
                pltpu.VMEM((states, states), f32),
                pltpu.VMEM((states, states), bf16),
                pltpu.VMEM((states, states), bf16),
                pltpu.VMEM((5, states, states), bf16),
                pltpu.VMEM((5, n_tiles * half, states), bf16),
                pltpu.VMEM((n_tiles * half, states), f32),
                pltpu.VMEM((NMOM, LANES), f32),
                pltpu.VMEM((count, 1, LANES), f32),
                pltpu.VMEM((count - 1, 1, LANES), f32),
                dma((SPLIT + 6,)),
            ] + [dma((CHUNKS,))] * 10 + [dma((count - 1,))] * 2 + [
                pltpu.VMEM((n_tiles, half, states), bf16), dma((n_tiles,))],
            compiler_params=pltpu.CompilerParams(
                collective_id=0, has_side_effects=True, vmem_limit_bytes=60 * 1024 * 1024
            ),
            name="measure_green",
        )(
            orders,
            momentum.reshape(n_pair, 1, half),
            frequency.reshape(1, states),
            vertex,
            left_phase,
            right_phase,
            tiles,
        )
        return chi, cells.reshape(-1)

    in_specs = (
        P("blk", "pair", None),
        P("blk", "pair", None),
        P("blk", None, None),
        P("blk", None, None),
        P("blk"),
        P(),
        P(),
    )
    out_specs = (P("blk", "pair", None), P(("blk", "pair")))
    return jax.shard_map(
        per_device, mesh=mesh, in_specs=in_specs, out_specs=out_specs, check_vma=False
    )
```

profile of v0, /device:TPU:0, one launch (start us, length us, event | category | flops | bytes accessed | tf_op | source)
XLA Modules:
  0.0 45.1 jit_solution(5502356341065239709)
XLA Ops:
  1.3 41.0 %measure_green.1 = (bf16[4,256,512]{2,1,0:T(8,128)(2,1)}, f32[1,64]{1,0:T(1,128)}) custom-call(s32[1]{0:T(128)S(6)} %copy.11.refs_0_, s32[2,1,256]{2,1,0:T(1,128)} %bitcast.3, s32[1,512]{1,0:T(1,128)} %bitcast.4, bf16[1,1024,2048]{2,1,0:T(8,128)(2,1)} %refs_3_.1, bf16[1,1024,512]{2,1,0:T(8,128)(2,1)} %refs_4_.1, bf16[1,2048,512]{2,1,0:T(8,128)(2,1)} %refs_5_.1, ...), custom_call_target="tpu_custom_call" | custom-call | tf_op jit(solution)/shard_map/measure_green/pallas_call | solution.py:318
  42.3 0.0 copy-start
  42.3 2.3 %copy.12 = bf16[4,256,512]{2,1,0:T(8,128)(2,1)} copy(bf16[4,256,512]{2,1,0:T(8,128)(2,1)} %get-tuple-element.8) | data formatting | bytes 2097152
  44.6 0.0 copy-done
  44.6 0.5 %copy.13 = f32[64]{0:T(128)} copy(f32[64]{0:T(128)S(1)} %bitcast.5) | data formatting | bytes 512
Async XLA Ops:
  42.3 2.3 %copy-start = (f32[1,64]{1,0:T(1,128)S(1)}, f32[1,64]{1,0:T(1,128)}, u32[]{:S(2)}) copy-start(f32[1,64]{1,0:T(1,128)} %get-tuple-element.5) | copy-start | bytes 772
where the time goes:
time: 45.3 us; the launch traced here: 45.1 us
  Pallas kernels  41 us (91%)
  local copies, waits for them, and re-layouts  2.78 us (6%)
  between operations  1.29 us (3%)
    pallas_call x1, Pallas kernels, per_device(): pl.pallas_call(lambda *refs: body(sizes, *refs), out_shape=(jax.ShapeDtyp...  41 us
    unnamed x4, local copies, waits for them, and re-layouts  2.78 us

commit v1 on v0

v1 whole, which is shorter than its diff:
```python
import math

import jax
import jax.numpy as jnp
from jax import lax
from jax.experimental import pallas as pl
from jax.experimental.pallas import tpu as pltpu
from jax.sharding import PartitionSpec as P

NMOM = 64
NFREQ = 32
LANES = 128
SIZE = 128
SPLIT = 2
MESH = pl.DeviceIdType.MESH
OWN, PEER, ACROSS, RELAYED, FORWARDED = range(5)

FIRST, HOP, NEAR, STEP = 7.2, 1.7, 1.0, 1.41
INNER, CHI = 0.5, 0.25


def contract(a, b, dims, precision=None):
    return lax.dot_general(
        a, b, (dims, ((), ())), preferred_element_type=jnp.float32, precision=precision
    )


def plan(count):
    step = STEP * 8 / count
    half = count // 2
    quarter = count // 4
    arrive = {}
    for k in range(count):
        y = FIRST + step * (k + 1)
        arrive["y", k] = y
        arrive["x", k] = y + step + HOP
        arrive["z", k] = y + 2 * (step + HOP)
        arrive["p", k] = y + NEAR
        arrive["f", k] = arrive["z", k] + NEAR
    source = {OWN: "y", PEER: "p", ACROSS: "x", RELAYED: "z", FORWARDED: "f"}
    jobs = []
    for slot in range(5):
        s = source[slot]
        for part in range(2):
            jobs.append((arrive[s, half - 1], INNER, ("inner", slot, part), [(s, half - 1)], []))
        for part in range(2):
            jobs.append((arrive[s, half - 1], CHI, ("own", slot, part), [(s, half - 1)],
                         [("inner", slot, part)]))
        for h in range(2):
            k = half + quarter * (h + 1) - 1
            if slot < RELAYED and h == 0:
                continue
            for part in range(2):
                length = CHI if slot < RELAYED else CHI / 2
                jobs.append((arrive[s, k], length, ("rest", slot, h, part), [(s, k)],
                             [("inner", slot, part)]))
    jobs.append((arrive["y", 1] + 0.5, 0.4, ("tiles", 0), [("y", 1)], []))
    jobs.append((arrive["y", 1] + 2.5, 0.3, ("tiles", 1), [("y", 1)], [("tiles", 0)]))
    jobs.append((arrive["y", count - 1], 0.3, ("cells", OWN), [("y", count - 1)], [("tiles", 1)]))
    jobs.append((arrive["x", count - 1], 0.3, ("cells", ACROSS), [("x", count - 1)],
                 [("cells", OWN)]))
    jobs.append((arrive["x", count - 1], 0.3, ("sigma",), [("x", count - 1)], [("cells", ACROSS)]))
    urgent = {"tiles": 0, "cells": 1, "sigma": 1, "inner": 2, "own": 3, "rest": 3}
    waits = sorted((t, key) for key, t in arrive.items() if key[0] in "yxz")
    order, done, now = [], set(), 0.0
    taken = set()
    while waits or jobs:
        if waits and waits[0][0] <= now + 0.1:
            t, key = waits.pop(0)
            now = max(now, t)
            order.append(key)
            taken.add(key)
            continue
        ready = [j for j in jobs if j[0] <= now and all(d in done for d in j[4])
                 and all(w in taken or w[0] in "pf" for w in j[3])]
        if ready:
            job = min(ready, key=lambda j: (urgent[j[2][0]], j[0]))
            jobs.remove(job)
            for w in job[3]:
                order.append(("need",) + w)
            order.append(job[2])
            done.add(job[2])
            now += job[1]
            continue
        times = [j[0] for j in jobs if j[0] > now] + ([waits[0][0]] if waits else [])
        now = min(times)
    return order


def body(sizes, order_ref, mom_ref, freq_ref, vertex_hbm, left_hbm, right_hbm, tiles_hbm,
         out_ref, sigma_ref,
         vertex, left, right, tiles, carried, partial, sending, arrived, greens, inner, acc,
         chi, tile_sum, tile_send, tile_recv, back_send, back_recv, weight_own, weight_across,
         cells_ref, sig_send, sig_recv, load_sem, y_send, y_recv, x_send, x_recv, z_send, z_recv,
         p_send, p_recv, f_send, f_recv, w_send, t_send, t_recv, s_send, s_recv, o_sem, token):
    n_blk, n_pair, height, breadth, states, n_tiles = sizes
    count = n_blk * n_pair
    half = states // n_pair
    b = lax.axis_index("blk")
    p = lax.axis_index("pair")
    me = b * n_pair + p
    chip = b // 2
    core = lax.rem(b, 2)
    odd = lax.rem(chip, 2)
    step = 1 - 2 * odd
    across = (lax.rem(b + 2 * step + n_blk, n_blk), p)
    along = (lax.rem(b + 4 * step + n_blk, n_blk), p)
    back = (lax.rem(b - 4 * step + n_blk, n_blk), p)
    peer = (b + 1 - 2 * core, p)
    other = (b, 1 - p)
    forwards_across = lax.rem(odd + core, 2) == 0
    low_end = b < 4
    high_end = b >= n_blk - 4
    even = odd == 0
    wrap_send = jnp.logical_or(jnp.logical_and(even, high_end),
                               jnp.logical_and(jnp.logical_not(even), low_end))
    wrap_recv = jnp.logical_or(jnp.logical_and(even, low_end),
                               jnp.logical_and(jnp.logical_not(even), high_end))

    barrier = pltpu.get_barrier_semaphore()
    for device in (other, across, peer, along, back):
        pl.semaphore_signal(barrier, inc=1, device_id=device, device_id_type=MESH)

    pieces = 4
    block = height // pieces
    wide = states // SPLIT

    def load_right(h):
        cols = pl.ds(h * wide, wide)
        return pltpu.make_async_copy(right_hbm.at[0, :, cols], right.at[h], load_sem.at[h])

    load_right(0).start()
    load_vertex = []
    for i in range(pieces):
        rows = pl.ds(i * block, block)
        copy = pltpu.make_async_copy(vertex_hbm.at[0, rows], vertex.at[rows], load_sem.at[SPLIT + i])
        copy.start()
        load_vertex.append(copy)
    load_left = pltpu.make_async_copy(left_hbm.at[0], left, load_sem.at[SPLIT + pieces])
    load_left.start()
    for h in range(1, SPLIT):
        load_right(h).start()
    load_tiles = pltpu.make_async_copy(tiles_hbm, tiles, load_sem.at[SPLIT + 1 + pieces])
    load_tiles.start()

    order = order_ref[0]
    scale = 1.0 / math.sqrt(breadth)
    per = half // SIZE
    total = n_pair * SPLIT * per
    middle = total // 2

    def chunk(which, k):
        group, h, i = k // (SPLIT * per), k // per % SPLIT, k % per
        start = lax.rem(which + group, n_pair) * half + i * SIZE
        return pl.ds(pl.multiple_of(start, SIZE), SIZE), pl.ds(h * wide, wide)

    def remote(src, dst, send, recv, device):
        return pltpu.make_async_remote_copy(src_ref=src, dst_ref=dst, send_sem=send, recv_sem=recv,
                                            device_id=device, device_id_type=MESH)

    def exchange(k, which):
        rows = chunk(which, k)
        return remote(sending.at[*rows], arrived.at[*rows], y_send.at[k], y_recv.at[k], other)

    def hop(source, target, k, send, recv, device):
        rows = chunk(p, k)
        return remote(greens.at[source, *rows], greens.at[target, *rows], send, recv, device)

    def to_across(k):
        return hop(OWN, ACROSS, k, x_send.at[k], x_recv.at[k], across)

    def to_peer(k):
        return hop(OWN, PEER, k, p_send.at[k], p_recv.at[k], peer)

    def to_along(k):
        return hop(ACROSS, RELAYED, k, z_send.at[k], z_recv.at[k], along)

    def to_other(k):
        return hop(RELAYED, RELAYED, k, w_send.at[k], z_recv.at[k + middle], other)

    def forward(source, k):
        return hop(source, FORWARDED, k, f_send.at[k], f_recv.at[k], peer)

    def send_tiles():
        return remote(tile_send, tile_recv, t_send.at[0], t_recv.at[0], peer)

    def send_back():
        return remote(back_send, back_recv, t_send.at[1], t_recv.at[1], back)

    ring = n_blk // 4
    rounds = 3 + max(ring // 2 - 1, 0)

    def near(r):
        return (other, across, peer) if r < 3 else (along, back)

    def give(r):
        for device in near(r):
            pl.semaphore_signal(token.at[r], inc=1, device_id=device, device_id_type=MESH)

    def take(r):
        pl.semaphore_wait(token.at[r], len(near(r)))

    def mask_right(h):
        def part(i, carry):
            rows = pl.ds(pl.multiple_of(i * 256, 256), 256)
            ids = i * 256 + lax.broadcasted_iota(jnp.int32, (256, wide), 0)
            right[h, rows, :] = jnp.where(ids < order, right[h, rows, :],
                                          jnp.zeros((), jnp.bfloat16))
            return carry

        lax.fori_loop(0, breadth // 256, part, 0)

    def carry_half(h):
        for i in range(pieces):
            rows = pl.ds(i * block, block)
            if h == 0:
                load_vertex[i].wait()
            product = contract(vertex[rows, :], right[h], ((1,), (0,)))
            ids = p * height + i * block + lax.broadcasted_iota(jnp.int32, (block, wide), 0)
            carried[h, rows, :] = jnp.where(ids < order, product, 0.0).astype(jnp.bfloat16)

    def partial_block(group, h):
        which = lax.rem(1 - p + group, n_pair)
        rows = pl.ds(pl.multiple_of(which * half, half), half)
        cols = pl.ds(h * wide, wide)
        product = contract(left[:, rows], carried[h], ((0,), (0,))) * scale
        partial[rows, cols] = product
        sending[rows, cols] = product.astype(jnp.bfloat16)
        for i in range(per):
            exchange((group * SPLIT + h) * per + i, 1 - p).start()

    load_right(0).wait()
    mask_right(0)
    carry_half(0)
    load_left.wait()
    pl.semaphore_wait(barrier, 5)
    partial_block(0, 0)
    give(0)
    for h in range(1, SPLIT):
        load_right(h).wait()
        mask_right(h)
        carry_half(h)
        partial_block(0, h)
    for group in range(1, n_pair):
        for h in range(SPLIT):
            partial_block(group, h)

    ids_m = lax.broadcasted_iota(jnp.int32, (NMOM, states), 0)
    pick_mom = (ids_m == mom_ref[...]).astype(jnp.bfloat16)
    ids_f = lax.broadcasted_iota(jnp.int32, (LANES, states), 0)
    pick_freq = (ids_f == freq_ref[...]).astype(jnp.bfloat16)
    own_rows = pl.ds(pl.multiple_of(p * half, half), half)
    rest_rows = pl.ds(pl.multiple_of((1 - p) * half, half), half)
    out_scale = 1.0 / math.sqrt(states)
    pair_share = forwards_across.astype(jnp.float32)

    load_tiles.wait()

    def tile_stage(stage):
        if stage == 0:
            value = tiles[0, own_rows, :].astype(jnp.float32)
            for t in range(1, n_tiles):
                value = value + tiles[t, own_rows, :].astype(jnp.float32)
            tile_sum[...] = value
            tile_send[...] = value.astype(jnp.bfloat16)
            send_tiles().start()
        else:
            send_tiles().wait_recv()
            mine = tile_sum[...]
            theirs = tile_recv[...].astype(jnp.float32)
            back_send[...] = (mine + (1.0 - pair_share) * theirs).astype(jnp.bfloat16)
            send_back().start()
            weight_own[...] = (mine + theirs).astype(jnp.bfloat16)
            tile_sum[...] = mine + pair_share * theirs

    def cells(slot):
        if slot == ACROSS:
            send_back().wait_recv()
            weight_across[...] = (
                tile_sum[...] + back_recv[...].astype(jnp.float32)
            ).astype(jnp.bfloat16)
        weight = weight_own if slot == OWN else weight_across
        folded = contract(pick_mom, greens[slot], ((1,), (0,)))
        folded = jnp.where(p == 0, folded[:, :half], folded[:, half:])
        high = folded.astype(jnp.bfloat16)
        low = (folded - high.astype(jnp.float32)).astype(jnp.bfloat16)
        joined = (contract(high, weight[...], ((1,), (0,)))
                  + contract(low, weight[...], ((1,), (0,))))
        picked = contract(pick_freq, greens[slot], ((1,), (0,)))
        value = contract(joined, picked, ((1,), (1,)), lax.Precision.HIGHEST)
        cells_ref[...] = value if slot == OWN else cells_ref[...] + value

    own_cells = NMOM * NFREQ // count

    def owner(i):
        to = lax.rem(me + i, count)
        return remote(sig_send.at[to], sig_recv.at[i - 1], s_send.at[i - 1], s_recv.at[i - 1],
                      (to // n_pair, lax.rem(to, n_pair)))

    def sigma():
        value_cells = cells_ref[...]
        rows_d = lax.broadcasted_iota(jnp.int32, (count, NMOM), 0)
        cols_m = lax.broadcasted_iota(jnp.int32, (count, NMOM), 1)
        spread = jnp.zeros((count, LANES), jnp.float32)
        if own_cells >= NFREQ:
            group = own_cells // NFREQ
            for k in range(group):
                pick = (cols_m == rows_d * group + k).astype(jnp.float32)
                value = contract(pick, value_cells, ((1,), (0,)), lax.Precision.HIGHEST)
                spread = spread + (pltpu.roll(value, NFREQ * k, 1) if k else value)
        else:
            group = NFREQ // own_cells
            for k in range(group):
                pick = (rows_d == cols_m * group + k).astype(jnp.float32)
                value = contract(pick, value_cells, ((1,), (0,)), lax.Precision.HIGHEST)
                spread = spread + (pltpu.roll(value, LANES - own_cells * k, 1) if k else value)
        factor = 1.0 / math.sqrt(5.0 * n_tiles * n_blk * states * states / (NMOM * NFREQ))
        sig_send[...] = (spread * (factor * out_scale)).reshape(count, 1, LANES)

        def send_cells(i, carry):
            owner(i).start()
            return carry

        lax.fori_loop(1, count, send_cells, 0)

    share = n_tiles // 2

    def compute_inner(slot, part):
        upper = greens[slot, own_rows, :]
        for t in range(part * share, (part + 1) * share):
            inner[slot, pl.ds(t * half, half), :] = contract(
                upper, tiles[t], ((1,), (0,))).astype(jnp.bfloat16)

    started = set()
    pending = {(0, part): 5 for part in range(2)} | {(1, part): 7 for part in range(2)}

    def store(group, t):
        rows = own_rows if group == 0 else rest_rows
        return pltpu.make_async_copy(chi.at[group, t], out_ref.at[t, :, rows],
                                     o_sem.at[group, t])

    def compute_chi(group, slot, part, k_half=None):
        rows = own_rows if group == 0 else rest_rows
        cols = pl.ds(0, states) if k_half is None else pl.ds(k_half * wide, wide)
        first = (group, part) not in started
        started.add((group, part))
        pending[group, part] -= 1
        last = pending[group, part] == 0
        for t in range(part * share, (part + 1) * share):
            lines = pl.ds(t * half, half)
            value = contract(inner[slot, lines, cols], greens[slot, rows, cols], ((1,), (1,)))
            if not first:
                value = acc[group, lines, :] + value
            if last:
                chi[group, t] = (value * out_scale).astype(jnp.bfloat16)
                store(group, t).start()
            else:
                acc[group, lines, :] = value

    def take_y(k):
        rows = chunk(p, k)
        exchange(k, p).wait_recv()
        greens[OWN, *rows] = (
            partial[*rows] + arrived[*rows].astype(jnp.float32)
        ).astype(jnp.bfloat16)
        to_across(k).start()
        to_peer(k).start()

    def take_x(k):
        to_across(k).wait_recv()
        if k < middle:
            to_along(k).start()
        else:
            @pl.when(jnp.logical_not(wrap_send))
            def _():
                to_along(k).start()

        @pl.when(forwards_across)
        def _():
            forward(ACROSS, k).start()

    def take_z(k):
        to_along(k).wait_recv()
        if k < middle:
            @pl.when(wrap_recv)
            def _():
                to_other(k).start()

        @pl.when(jnp.logical_not(forwards_across))
        def _():
            forward(RELAYED, k).start()

    waited = {"p": 0, "f": 0}

    def need(kind, k):
        if kind in waited:
            while waited[kind] <= k:
                at = waited[kind]
                (to_peer(at) if kind == "p" else forward(ACROSS, at)).wait_recv()
                waited[kind] += 1

    passed = 0
    for task in plan(total):
        kind = task[0]
        if kind == "y":
            take_y(task[1])
        elif kind == "x":
            take_x(task[1])
            if passed < rounds - 1:
                take(passed)
                passed += 1
                give(passed)
        elif kind == "z":
            take_z(task[1])
        elif kind == "need":
            need(task[1], task[2])
        elif kind == "tiles":
            tile_stage(task[1])
        elif kind == "cells":
            cells(task[1])
        elif kind == "sigma":
            while passed < rounds - 1:
                take(passed)
                passed += 1
                give(passed)
            take(passed)
            sigma()
        elif kind == "inner":
            compute_inner(task[1], task[2])
        elif kind == "own":
            compute_chi(0, task[1], task[2])
        elif kind == "rest":
            compute_chi(1, task[1], task[3], None if task[1] < RELAYED else task[2])

    for k in range(total):
        exchange(k, 1 - p).wait_send()
        to_across(k).wait_send()
        to_peer(k).wait_send()
        forward(ACROSS, k).wait_send()
        if k < middle:
            to_along(k).wait_send()

            @pl.when(wrap_recv)
            def _():
                to_other(k).wait_send()
        else:
            @pl.when(jnp.logical_not(wrap_send))
            def _():
                to_along(k).wait_send()
    send_tiles().wait_send()
    send_back().wait_send()

    def take_cells(i, carry):
        owner(i).wait()
        return carry

    lax.fori_loop(1, count, take_cells, 0)
    summed = jnp.sum(sig_recv[...], axis=0) + sig_send[me]
    sigma_ref[...] = summed[:, :own_cells]
    for group in range(2):
        for t in range(n_tiles):
            store(group, t).wait()


def solution(mesh):
    n_blk, n_pair = mesh.shape["blk"], mesh.shape["pair"]
    count = n_blk * n_pair

    def per_device(vertex, left_phase, right_phase, tiles, orders, momentum, frequency):
        height, breadth = vertex.shape[1], vertex.shape[2]
        states = right_phase.shape[2]
        n_tiles = tiles.shape[0]
        half = states // n_pair
        sizes = (n_blk, n_pair, height, breadth, states, n_tiles)
        bf16, f32 = jnp.bfloat16, jnp.float32
        dma = pltpu.SemaphoreType.DMA
        chunks = n_pair * SPLIT * (half // SIZE)
        rounds = 3 + max(n_blk // 4 // 2 - 1, 0)
        chi, cells = pl.pallas_call(
            lambda *refs: body(sizes, *refs),
            out_shape=(
                jax.ShapeDtypeStruct((n_tiles, half, states), bf16),
                jax.ShapeDtypeStruct((1, NMOM * NFREQ // count), f32),
            ),
            in_specs=[
                pl.BlockSpec(memory_space=pltpu.SMEM),
                pl.BlockSpec(memory_space=pltpu.VMEM),
                pl.BlockSpec(memory_space=pltpu.VMEM),
            ] + [pl.BlockSpec(memory_space=pltpu.HBM)] * 4,
            out_specs=(
                pl.BlockSpec(memory_space=pltpu.HBM),
                pl.BlockSpec(memory_space=pltpu.VMEM),
            ),
            scratch_shapes=[
                pltpu.VMEM((height, breadth), bf16),
                pltpu.VMEM((height, states), bf16),
                pltpu.VMEM((SPLIT, breadth, states // SPLIT), bf16),
                pltpu.VMEM((n_tiles, states, states), bf16),
                pltpu.VMEM((SPLIT, height, states // SPLIT), bf16),
                pltpu.VMEM((states, states), f32),
                pltpu.VMEM((states, states), bf16),
                pltpu.VMEM((states, states), bf16),
                pltpu.VMEM((5, states, states), bf16),
                pltpu.VMEM((5, n_tiles * half, states), bf16),
                pltpu.VMEM((2, n_tiles * half, half), f32),
                pltpu.VMEM((2, n_tiles, half, half), bf16),
                pltpu.VMEM((half, states), f32),
            ] + [pltpu.VMEM((half, states), bf16)] * 6 + [
                pltpu.VMEM((NMOM, LANES), f32),
                pltpu.VMEM((count, 1, LANES), f32),
                pltpu.VMEM((count - 1, 1, LANES), f32),
                dma((SPLIT + 6,)),
            ] + [dma((chunks,))] * 11 + [dma((2,))] * 2 + [dma((count - 1,))] * 2 + [
                dma((2, n_tiles)), pltpu.SemaphoreType.REGULAR((rounds,))],
            compiler_params=pltpu.CompilerParams(
                collective_id=0, has_side_effects=True, vmem_limit_bytes=60 * 1024 * 1024
            ),
            name="measure_green",
        )(
            orders,
            momentum.reshape(1, states),
            frequency.reshape(1, states),
            vertex,
            left_phase,
            right_phase,
            tiles,
        )
        return chi, cells.reshape(-1)

    in_specs = (
        P("blk", "pair", None),
        P("blk", "pair", None),
        P("blk", None, None),
        P("blk", None, None),
        P("blk"),
        P(),
        P(),
    )
    out_specs = (P("blk", "pair", None), P(("blk", "pair")))
    return jax.shard_map(
        per_device, mesh=mesh, in_specs=in_specs, out_specs=out_specs, check_vma=False
    )
```

time: 45.3 us -> 44.4 us (0.980)
  Pallas kernels: 41 us -> 40.1 us
    pallas_call x1, Pallas kernels: 41 us -> 40.1 us  [per_device(): pl.pallas_call(lambda *refs: body(sizes, *refs), out_shape=(jax.ShapeDtyp...]
where the time goes in v1:
time: 44.4 us; the launch traced here: 44.2 us
  Pallas kernels  40.1 us (90%)
  local copies, waits for them, and re-layouts  2.78 us (6%)
  between operations  1.29 us (3%)
    pallas_call x1, Pallas kernels, per_device(): pl.pallas_call(lambda *refs: body(sizes, *refs), out_shape=(jax.ShapeDtyp...  40.1 us
    unnamed x4, local copies, waits for them, and re-layouts  2.78 us

profile of v1, /device:TPU:0, one launch (start us, length us, event | category | flops | bytes accessed | tf_op | source)
XLA Modules:
  0.0 44.2 jit_solution(7427201552696544870)
XLA Ops:
  1.3 40.1 %measure_green.1 = (bf16[4,256,512]{2,1,0:T(8,128)(2,1)}, f32[1,64]{1,0:T(1,128)}) custom-call(s32[1]{0:T(128)S(6)} %copy.11.refs_0_, s32[1,512]{1,0:T(1,128)} %bitcast.3, s32[1,512]{1,0:T(1,128)} %bitcast.4, bf16[1,1024,2048]{2,1,0:T(8,128)(2,1)} %refs_3_.1, bf16[1,1024,512]{2,1,0:T(8,128)(2,1)} %refs_4_.1, bf16[1,2048,512]{2,1,0:T(8,128)(2,1)} %refs_5_.1, ...), custom_call_target="tpu_custom_call" | custom-call | tf_op jit(solution)/shard_map/measure_green/pallas_call | solution.py:479
  41.4 0.0 copy-start
  41.4 2.3 %copy.12 = bf16[4,256,512]{2,1,0:T(8,128)(2,1)} copy(bf16[4,256,512]{2,1,0:T(8,128)(2,1)} %get-tuple-element.8) | data formatting | bytes 2097152
  43.7 0.0 copy-done
  43.7 0.5 %copy.13 = f32[64]{0:T(128)} copy(f32[64]{0:T(128)S(1)} %bitcast.5) | data formatting | bytes 512
Async XLA Ops:
  41.4 2.3 %copy-start = (f32[1,64]{1,0:T(1,128)S(1)}, f32[1,64]{1,0:T(1,128)}, u32[]{:S(2)}) copy-start(f32[1,64]{1,0:T(1,128)} %get-tuple-element.5) | copy-start | bytes 772

commit v2 on v1

--- a/solution.py
+++ b/solution.py
@@ -12,6 +12,7 @@
 LANES = 128
 SIZE = 128
 SPLIT = 2
+PIECES = 8
 MESH = pl.DeviceIdType.MESH
 OWN, PEER, ACROSS, RELAYED, FORWARDED = range(5)
 
@@ -54,13 +55,11 @@
                 length = CHI if slot < RELAYED else CHI / 2
                 jobs.append((arrive[s, k], length, ("rest", slot, h, part), [(s, k)],
                              [("inner", slot, part)]))
-    jobs.append((arrive["y", 1] + 0.5, 0.4, ("tiles", 0), [("y", 1)], []))
-    jobs.append((arrive["y", 1] + 2.5, 0.3, ("tiles", 1), [("y", 1)], [("tiles", 0)]))
-    jobs.append((arrive["y", count - 1], 0.3, ("cells", OWN), [("y", count - 1)], [("tiles", 1)]))
+    jobs.append((arrive["y", count - 1], 0.3, ("cells", OWN), [("y", count - 1)], []))
     jobs.append((arrive["x", count - 1], 0.3, ("cells", ACROSS), [("x", count - 1)],
                  [("cells", OWN)]))
     jobs.append((arrive["x", count - 1], 0.3, ("sigma",), [("x", count - 1)], [("cells", ACROSS)]))
-    urgent = {"tiles": 0, "cells": 1, "sigma": 1, "inner": 2, "own": 3, "rest": 3}
+    urgent = {"cells": 1, "sigma": 1, "inner": 2, "own": 3, "rest": 3}
     waits = sorted((t, key) for key, t in arrive.items() if key[0] in "yxz")
     order, done, now = [], set(), 0.0
     taken = set()
@@ -87,12 +86,12 @@
     return order
 
 
-def body(sizes, order_ref, mom_ref, freq_ref, vertex_hbm, left_hbm, right_hbm, tiles_hbm,
+def body(sizes, order_hbm, mom_hbm, freq_hbm, vertex_hbm, left_hbm, right_hbm, tiles_hbm,
          out_ref, sigma_ref,
-         vertex, left, right, tiles, carried, partial, sending, arrived, greens, inner, acc,
-         chi, tile_sum, tile_send, tile_recv, back_send, back_recv, weight_own, weight_across,
+         order_ref, mom_ref, freq_ref, small_sem, vertex, left, turned, right, tiles, carried, partial, sending, arrived, greens, inner, acc,
+         tile_sum, tile_send, tile_recv, back_send, back_recv, weight_own, weight_across,
          cells_ref, sig_send, sig_recv, load_sem, y_send, y_recv, x_send, x_recv, z_send, z_recv,
-         p_send, p_recv, f_send, f_recv, w_send, t_send, t_recv, s_send, s_recv, o_sem, token):
+         p_send, p_recv, f_send, f_recv, w_send, t_send, t_recv, s_send, s_recv, token):
     n_blk, n_pair, height, breadth, states, n_tiles = sizes
     count = n_blk * n_pair
     half = states // n_pair
@@ -118,10 +117,25 @@
                                jnp.logical_and(jnp.logical_not(even), high_end))
 
     barrier = pltpu.get_barrier_semaphore()
-    for device in (other, across, peer, along, back):
-        pl.semaphore_signal(barrier, inc=1, device_id=device, device_id_type=MESH)
-
-    pieces = 4
+
+    def tell(semaphore, devices):
+        for device in devices:
+            pl.semaphore_signal(semaphore, inc=1, device_id=device, device_id_type=MESH)
+
+    def tell_column(semaphore):
+        @pl.when(jnp.logical_not(wrap_send))
+        def _():
+            tell(semaphore, (along,))
+
+        @pl.when(jnp.logical_not(wrap_recv))
+        def _():
+            tell(semaphore, (back,))
+
+    beside = 2 - wrap_send.astype(jnp.int32) - wrap_recv.astype(jnp.int32)
+    tell(barrier, (other, across, peer))
+    tell_column(barrier)
+
+    pieces = PIECES
     block = height // pieces
     wide = states // SPLIT
 
@@ -129,21 +143,26 @@
         cols = pl.ds(h * wide, wide)
         return pltpu.make_async_copy(right_hbm.at[0, :, cols], right.at[h], load_sem.at[h])
 
-    load_right(0).start()
+    small = [
+        pltpu.make_async_copy(order_hbm, order_ref, small_sem.at[0]),
+        pltpu.make_async_copy(mom_hbm, mom_ref, small_sem.at[1]),
+        pltpu.make_async_copy(freq_hbm, freq_ref, small_sem.at[2]),
+    ]
+    load_left = pltpu.make_async_copy(left_hbm.at[0], left, load_sem.at[SPLIT + pieces])
+    load_tiles = pltpu.make_async_copy(tiles_hbm, tiles, load_sem.at[SPLIT + 1 + pieces])
     load_vertex = []
     for i in range(pieces):
         rows = pl.ds(i * block, block)
-        copy = pltpu.make_async_copy(vertex_hbm.at[0, rows], vertex.at[rows], load_sem.at[SPLIT + i])
+        load_vertex.append(
+            pltpu.make_async_copy(vertex_hbm.at[0, rows], vertex.at[rows], load_sem.at[SPLIT + i]))
+    small[0].start()
+    load_left.start()
+    load_right(0).start()
+    for copy in load_vertex:
         copy.start()
-        load_vertex.append(copy)
-    load_left = pltpu.make_async_copy(left_hbm.at[0], left, load_sem.at[SPLIT + pieces])
-    load_left.start()
-    for h in range(1, SPLIT):
-        load_right(h).start()
-    load_tiles = pltpu.make_async_copy(tiles_hbm, tiles, load_sem.at[SPLIT + 1 + pieces])
-    load_tiles.start()
-
-    order = order_ref[0]
+    for copy in small[1:]:
+        copy.start()
+
     scale = 1.0 / math.sqrt(breadth)
     per = half // SIZE
     total = n_pair * SPLIT * per
@@ -187,18 +206,17 @@
     def send_back():
         return remote(back_send, back_recv, t_send.at[1], t_recv.at[1], back)
 
-    ring = n_blk // 4
-    rounds = 3 + max(ring // 2 - 1, 0)
-
-    def near(r):
-        return (other, across, peer) if r < 3 else (along, back)
+    column = max(n_blk // 4 - 2, 0)
+    rounds = column + 2
 
     def give(r):
-        for device in near(r):
-            pl.semaphore_signal(token.at[r], inc=1, device_id=device, device_id_type=MESH)
+        if r < column:
+            tell_column(token.at[r])
+        else:
+            tell(token.at[r], (other, across, peer))
 
     def take(r):
-        pl.semaphore_wait(token.at[r], len(near(r)))
+        pl.semaphore_wait(token.at[r], beside if r < column else 3)
 
     def mask_right(h):
         def part(i, carry):
@@ -215,6 +233,9 @@
             rows = pl.ds(i * block, block)
             if h == 0:
                 load_vertex[i].wait()
+                if i == pieces // 2:
+                    load_right(1).start()
+                    load_tiles.start()
             product = contract(vertex[rows, :], right[h], ((1,), (0,)))
             ids = p * height + i * block + lax.broadcasted_iota(jnp.int32, (block, wide), 0)
             carried[h, rows, :] = jnp.where(ids < order, product, 0.0).astype(jnp.bfloat16)
@@ -223,38 +244,21 @@
         which = lax.rem(1 - p + group, n_pair)
         rows = pl.ds(pl.multiple_of(which * half, half), half)
         cols = pl.ds(h * wide, wide)
-        product = contract(left[:, rows], carried[h], ((0,), (0,))) * scale
+        product = contract(turned[group], carried[h], ((1,), (0,))) * scale
         partial[rows, cols] = product
         sending[rows, cols] = product.astype(jnp.bfloat16)
         for i in range(per):
             exchange((group * SPLIT + h) * per + i, 1 - p).start()
 
-    load_right(0).wait()
-    mask_right(0)
-    carry_half(0)
-    load_left.wait()
-    pl.semaphore_wait(barrier, 5)
-    partial_block(0, 0)
-    give(0)
-    for h in range(1, SPLIT):
-        load_right(h).wait()
-        mask_right(h)
-        carry_half(h)
-        partial_block(0, h)
-    for group in range(1, n_pair):
-        for h in range(SPLIT):
-            partial_block(group, h)
-
-    ids_m = lax.broadcasted_iota(jnp.int32, (NMOM, states), 0)
-    pick_mom = (ids_m == mom_ref[...]).astype(jnp.bfloat16)
-    ids_f = lax.broadcasted_iota(jnp.int32, (LANES, states), 0)
-    pick_freq = (ids_f == freq_ref[...]).astype(jnp.bfloat16)
+    def turn(group):
+        which = lax.rem(1 - p + group, n_pair)
+        cols = pl.ds(pl.multiple_of(which * half, half), half)
+        turned[group] = left[:, cols].T
+
     own_rows = pl.ds(pl.multiple_of(p * half, half), half)
     rest_rows = pl.ds(pl.multiple_of((1 - p) * half, half), half)
     out_scale = 1.0 / math.sqrt(states)
     pair_share = forwards_across.astype(jnp.float32)
-
-    load_tiles.wait()
 
     def tile_stage(stage):
         if stage == 0:
@@ -272,6 +276,41 @@
             send_back().start()
             weight_own[...] = (mine + theirs).astype(jnp.bfloat16)
             tile_sum[...] = mine + pair_share * theirs
+
+    small[0].wait()
+    order = order_ref[0]
+    load_left.wait()
+    turn(0)
+    load_right(0).wait()
+    mask_right(0)
+    carry_half(0)
+    pl.semaphore_wait(barrier, 3 + beside)
+    partial_block(0, 0)
+    passed = 0
+    give(passed)
+    load_tiles.wait()
+    tile_stage(0)
+    for h in range(1, SPLIT):
+        load_right(h).wait()
+        mask_right(h)
+        carry_half(h)
+        partial_block(0, h)
+    for passed in range(column):
+        take(passed)
+        give(passed + 1)
+    passed = column
+    tile_stage(1)
+    for group in range(1, n_pair):
+        turn(group)
+        for h in range(SPLIT):
+            partial_block(group, h)
+    for copy in small[1:]:
+        copy.wait()
+
+    ids_m = lax.broadcasted_iota(jnp.int32, (NMOM, states), 0)
+    pick_mom = (ids_m == mom_ref[...]).astype(jnp.bfloat16)
+    ids_f = lax.broadcasted_iota(jnp.int32, (LANES, states), 0)
+    pick_freq = (ids_f == freq_ref[...]).astype(jnp.bfloat16)
 
     def cells(slot):
         if slot == ACROSS:
@@ -334,11 +373,6 @@
     started = set()
     pending = {(0, part): 5 for part in range(2)} | {(1, part): 7 for part in range(2)}
 
-    def store(group, t):
-        rows = own_rows if group == 0 else rest_rows
-        return pltpu.make_async_copy(chi.at[group, t], out_ref.at[t, :, rows],
-                                     o_sem.at[group, t])
-
     def compute_chi(group, slot, part, k_half=None):
         rows = own_rows if group == 0 else rest_rows
         cols = pl.ds(0, states) if k_half is None else pl.ds(k_half * wide, wide)
@@ -352,8 +386,7 @@
             if not first:
                 value = acc[group, lines, :] + value
             if last:
-                chi[group, t] = (value * out_scale).astype(jnp.bfloat16)
-                store(group, t).start()
+                out_ref[t, :, rows] = (value * out_scale).astype(jnp.bfloat16)
             else:
                 acc[group, lines, :] = value
 
@@ -399,7 +432,6 @@
                 (to_peer(at) if kind == "p" else forward(ACROSS, at)).wait_recv()
                 waited[kind] += 1
 
-    passed = 0
     for task in plan(total):
         kind = task[0]
         if kind == "y":
@@ -414,8 +446,6 @@
             take_z(task[1])
         elif kind == "need":
             need(task[1], task[2])
-        elif kind == "tiles":
-            tile_stage(task[1])
         elif kind == "cells":
             cells(task[1])
         elif kind == "sigma":
@@ -456,10 +486,7 @@
 
     lax.fori_loop(1, count, take_cells, 0)
     summed = jnp.sum(sig_recv[...], axis=0) + sig_send[me]
-    sigma_ref[...] = summed[:, :own_cells]
-    for group in range(2):
-        for t in range(n_tiles):
-            store(group, t).wait()
+    sigma_ref[...] = summed[0, :own_cells]
 
 
 def solution(mesh):
@@ -475,25 +502,23 @@
         bf16, f32 = jnp.bfloat16, jnp.float32
         dma = pltpu.SemaphoreType.DMA
         chunks = n_pair * SPLIT * (half // SIZE)
-        rounds = 3 + max(n_blk // 4 // 2 - 1, 0)
+        rounds = max(n_blk // 4 - 2, 0) + 2
         chi, cells = pl.pallas_call(
             lambda *refs: body(sizes, *refs),
             out_shape=(
-                jax.ShapeDtypeStruct((n_tiles, half, states), bf16),
-                jax.ShapeDtypeStruct((1, NMOM * NFREQ // count), f32),
+                pltpu.VMEM((n_tiles, half, states), bf16),
+                pltpu.VMEM((NMOM * NFREQ // count,), f32),
             ),
-            in_specs=[
-                pl.BlockSpec(memory_space=pltpu.SMEM),
-                pl.BlockSpec(memory_space=pltpu.VMEM),
-                pl.BlockSpec(memory_space=pltpu.VMEM),
-            ] + [pl.BlockSpec(memory_space=pltpu.HBM)] * 4,
-            out_specs=(
-                pl.BlockSpec(memory_space=pltpu.HBM),
-                pl.BlockSpec(memory_space=pltpu.VMEM),
-            ),
+            in_specs=[pl.BlockSpec(memory_space=pltpu.HBM)] * 7,
+            out_specs=(pl.BlockSpec(memory_space=pltpu.VMEM),) * 2,
             scratch_shapes=[
+                pltpu.SMEM((1,), jnp.int32),
+                pltpu.VMEM((1, states), jnp.int32),
+                pltpu.VMEM((1, states), jnp.int32),
+                dma((3,)),
                 pltpu.VMEM((height, breadth), bf16),
                 pltpu.VMEM((height, states), bf16),
+                pltpu.VMEM((n_pair, half, height), bf16),
                 pltpu.VMEM((SPLIT, breadth, states // SPLIT), bf16),
                 pltpu.VMEM((n_tiles, states, states), bf16),
                 pltpu.VMEM((SPLIT, height, states // SPLIT), bf16),
@@ -503,15 +528,14 @@
                 pltpu.VMEM((5, states, states), bf16),
                 pltpu.VMEM((5, n_tiles * half, states), bf16),
                 pltpu.VMEM((2, n_tiles * half, half), f32),
-                pltpu.VMEM((2, n_tiles, half, half), bf16),
                 pltpu.VMEM((half, states), f32),
             ] + [pltpu.VMEM((half, states), bf16)] * 6 + [
                 pltpu.VMEM((NMOM, LANES), f32),
                 pltpu.VMEM((count, 1, LANES), f32),
                 pltpu.VMEM((count - 1, 1, LANES), f32),
-                dma((SPLIT + 6,)),
+                dma((SPLIT + PIECES + 2,)),
             ] + [dma((chunks,))] * 11 + [dma((2,))] * 2 + [dma((count - 1,))] * 2 + [
-                dma((2, n_tiles)), pltpu.SemaphoreType.REGULAR((rounds,))],
+                pltpu.SemaphoreType.REGULAR((rounds,))],
             compiler_params=pltpu.CompilerParams(
                 collective_id=0, has_side_effects=True, vmem_limit_bytes=60 * 1024 * 1024
             ),
@@ -525,7 +549,7 @@
             right_phase,
             tiles,
         )
-        return chi, cells.reshape(-1)
+        return chi, cells
 
     in_specs = (
         P("blk", "pair", None),

time: 44.4 us -> 39.6 us (0.89)
  Pallas kernels: 40.1 us -> 36.7 us
  local copies, waits for them, and re-layouts: 2.78 us -> 1.48 us
    pallas_call x1, Pallas kernels: 40.1 us -> 36.7 us  [per_device(): pl.pallas_call(lambda *refs: body(sizes, *refs), out_shape=(pltpu.VMEM((n...]
    unnamed x4 -> x2, local copies, waits for them, and re-layouts: 2.78 us -> 1.48 us
where the time goes in v2:
time: 39.6 us; the launch traced here: 39.4 us
  Pallas kernels  36.7 us (93%)
  local copies, waits for them, and re-layouts  1.48 us (4%)
  between operations  1.29 us (3%)
    pallas_call x1, Pallas kernels, per_device(): pl.pallas_call(lambda *refs: body(sizes, *refs), out_shape=(pltpu.VMEM((n...  36.7 us
    unnamed x2, local copies, waits for them, and re-layouts  1.48 us

profile of v2, /device:TPU:0, one launch (start us, length us, event | category | flops | bytes accessed | tf_op | source)
XLA Modules:
  0.0 39.4 jit_solution(53833149269471688)
XLA Ops:
  1.3 36.7 %measure_green.1 = (bf16[4,256,512]{2,1,0:T(8,128)(2,1)S(1)}, f32[64]{0:T(128)S(1)}) custom-call(s32[1]{0:T(128)S(6)} %copy.13.refs_0_, s32[1,512]{1,0:T(1,128)} %bitcast.2, s32[1,512]{1,0:T(1,128)} %bitcast.3, bf16[1,1024,2048]{2,1,0:T(8,128)(2,1)} %refs_3_.1, bf16[1,1024,512]{2,1,0:T(8,128)(2,1)} %refs_4_.1, bf16[1,2048,512]{2,1,0:T(8,128)(2,1)} %refs_5_.1, ...), custom_call_target="tpu_custom_call" | custom-call | tf_op jit(solution)/shard_map/measure_green/pallas_call | solution.py:506
  37.9 1.0 %copy.11 = bf16[4,256,512]{2,1,0:T(8,128)(2,1)} copy(bf16[4,256,512]{2,1,0:T(8,128)(2,1)S(1)} %get-tuple-element.2) | data formatting | bytes 2097152
  38.9 0.5 %copy.12 = f32[64]{0:T(128)} copy(f32[64]{0:T(128)S(1)} %get-tuple-element.3) | data formatting | bytes 512

commit v3 on v2

--- a/solution.py
+++ b/solution.py
@@ -16,8 +16,8 @@
 MESH = pl.DeviceIdType.MESH
 OWN, PEER, ACROSS, RELAYED, FORWARDED = range(5)
 
-FIRST, HOP, NEAR, STEP = 7.2, 1.7, 1.0, 1.41
-INNER, CHI = 0.5, 0.25
+FIRST, HOP, NEAR, LATE, LAST, STEP = 8.2, 1.9, 1.0, 3.0, 4.0, 1.41
+INNER, CHI = 0.2, 0.11
 
 
 def contract(a, b, dims, precision=None):
@@ -26,7 +26,7 @@
     )
 
 
-def plan(count):
+def plan(count, parts):
     step = STEP * 8 / count
     half = count // 2
     quarter = count // 4
@@ -35,23 +35,26 @@
         y = FIRST + step * (k + 1)
         arrive["y", k] = y
         arrive["x", k] = y + step + HOP
-        arrive["z", k] = y + 2 * (step + HOP)
+        arrive["z", k] = y + 2 * (step + HOP) + (LATE if k < half else max(LAST - LATE, 0.0))
         arrive["p", k] = y + NEAR
+    for k in range(half, count):
+        arrive["z", k] = max(arrive["z", k], arrive["z", k - half] + step + HOP)
+    for k in range(count):
         arrive["f", k] = arrive["z", k] + NEAR
     source = {OWN: "y", PEER: "p", ACROSS: "x", RELAYED: "z", FORWARDED: "f"}
     jobs = []
     for slot in range(5):
         s = source[slot]
-        for part in range(2):
+        for part in range(parts):
             jobs.append((arrive[s, half - 1], INNER, ("inner", slot, part), [(s, half - 1)], []))
-        for part in range(2):
+        for part in range(parts):
             jobs.append((arrive[s, half - 1], CHI, ("own", slot, part), [(s, half - 1)],
                          [("inner", slot, part)]))
         for h in range(2):
             k = half + quarter * (h + 1) - 1
             if slot < RELAYED and h == 0:
                 continue
-            for part in range(2):
+            for part in range(parts):
                 length = CHI if slot < RELAYED else CHI / 2
                 jobs.append((arrive[s, k], length, ("rest", slot, h, part), [(s, k)],
                              [("inner", slot, part)]))
@@ -64,7 +67,7 @@
     order, done, now = [], set(), 0.0
     taken = set()
     while waits or jobs:
-        if waits and waits[0][0] <= now + 0.1:
+        if waits and waits[0][0] <= now + 0.05:
             t, key = waits.pop(0)
             now = max(now, t)
             order.append(key)
@@ -155,13 +158,17 @@
         rows = pl.ds(i * block, block)
         load_vertex.append(
             pltpu.make_async_copy(vertex_hbm.at[0, rows], vertex.at[rows], load_sem.at[SPLIT + i]))
+    queue = list(load_vertex) + [load_right(h) for h in range(1, SPLIT)] + [load_tiles] + small[1:]
+
+    def pump(number):
+        for copy in queue[:number]:
+            copy.start()
+        del queue[:number]
+
     small[0].start()
     load_left.start()
     load_right(0).start()
-    for copy in load_vertex:
-        copy.start()
-    for copy in small[1:]:
-        copy.start()
+    pump(3)
 
     scale = 1.0 / math.sqrt(breadth)
     per = half // SIZE
@@ -179,26 +186,26 @@
 
     def exchange(k, which):
         rows = chunk(which, k)
-        return remote(sending.at[*rows], arrived.at[*rows], y_send.at[k], y_recv.at[k], other)
+        return remote(sending.at[*rows], arrived.at[*rows], y_send.at[0], y_recv.at[k], other)
 
     def hop(source, target, k, send, recv, device):
         rows = chunk(p, k)
         return remote(greens.at[source, *rows], greens.at[target, *rows], send, recv, device)
 
     def to_across(k):
-        return hop(OWN, ACROSS, k, x_send.at[k], x_recv.at[k], across)
+        return hop(OWN, ACROSS, k, x_send.at[0], x_recv.at[k], across)
 
     def to_peer(k):
-        return hop(OWN, PEER, k, p_send.at[k], p_recv.at[k], peer)
+        return hop(OWN, PEER, k, p_send.at[0], p_recv.at[k], peer)
 
     def to_along(k):
-        return hop(ACROSS, RELAYED, k, z_send.at[k], z_recv.at[k], along)
+        return hop(ACROSS, RELAYED, k, z_send.at[k // middle], z_recv.at[k], along)
 
     def to_other(k):
-        return hop(RELAYED, RELAYED, k, w_send.at[k], z_recv.at[k + middle], other)
+        return hop(RELAYED, RELAYED, k, w_send.at[0], z_recv.at[k + middle], other)
 
     def forward(source, k):
-        return hop(source, FORWARDED, k, f_send.at[k], f_recv.at[k], peer)
+        return hop(source, FORWARDED, k, f_send.at[0], f_recv.at[k], peer)
 
     def send_tiles():
         return remote(tile_send, tile_recv, t_send.at[0], t_recv.at[0], peer)
@@ -233,12 +240,26 @@
             rows = pl.ds(i * block, block)
             if h == 0:
                 load_vertex[i].wait()
-                if i == pieces // 2:
-                    load_right(1).start()
-                    load_tiles.start()
+                pump(1)
             product = contract(vertex[rows, :], right[h], ((1,), (0,)))
             ids = p * height + i * block + lax.broadcasted_iota(jnp.int32, (block, wide), 0)
             carried[h, rows, :] = jnp.where(ids < order, product, 0.0).astype(jnp.bfloat16)
+            if h == 0 and i % 2 == 1:
+                first_block(i // 2)
+
+    def first_block(i):
+        rows = pl.ds(pl.multiple_of((1 - p) * half, half), half)
+        depth = pl.ds(2 * i * block, 2 * block)
+        product = contract(turned[0, :, depth], carried[0, depth, :], ((1,), (0,))) * scale
+        if i > 0:
+            product = partial[rows, pl.ds(0, wide)] + product
+        partial[rows, pl.ds(0, wide)] = product
+        if i == pieces // 2 - 1:
+            sending[rows, pl.ds(0, wide)] = product.astype(jnp.bfloat16)
+
+    def send_block(group, h):
+        for i in range(per):
+            exchange((group * SPLIT + h) * per + i, 1 - p).start()
 
     def partial_block(group, h):
         which = lax.rem(1 - p + group, n_pair)
@@ -247,8 +268,7 @@
         product = contract(turned[group], carried[h], ((1,), (0,))) * scale
         partial[rows, cols] = product
         sending[rows, cols] = product.astype(jnp.bfloat16)
-        for i in range(per):
-            exchange((group * SPLIT + h) * per + i, 1 - p).start()
+        send_block(group, h)
 
     def turn(group):
         which = lax.rem(1 - p + group, n_pair)
@@ -280,12 +300,15 @@
     small[0].wait()
     order = order_ref[0]
     load_left.wait()
+    pump(2)
     turn(0)
     load_right(0).wait()
+    pump(2)
     mask_right(0)
     carry_half(0)
+    pump(len(queue))
     pl.semaphore_wait(barrier, 3 + beside)
-    partial_block(0, 0)
+    send_block(0, 0)
     passed = 0
     give(passed)
     load_tiles.wait()
@@ -307,10 +330,18 @@
     for copy in small[1:]:
         copy.wait()
 
+    own_cells = NMOM * NFREQ // count
+    folds = max(own_cells // NFREQ, 1)
     ids_m = lax.broadcasted_iota(jnp.int32, (NMOM, states), 0)
+    ids_m = lax.rem(ids_m, NMOM // folds) * folds + ids_m // (NMOM // folds)
     pick_mom = (ids_m == mom_ref[...]).astype(jnp.bfloat16)
     ids_f = lax.broadcasted_iota(jnp.int32, (LANES, states), 0)
     pick_freq = (ids_f == freq_ref[...]).astype(jnp.bfloat16)
+
+    def split(value):
+        high = value.astype(jnp.bfloat16)
+        low = (value - high.astype(jnp.float32)).astype(jnp.bfloat16)
+        return jnp.concatenate([high, low], axis=0)
 
     def cells(slot):
         if slot == ACROSS:
@@ -321,19 +352,17 @@
         weight = weight_own if slot == OWN else weight_across
         folded = contract(pick_mom, greens[slot], ((1,), (0,)))
         folded = jnp.where(p == 0, folded[:, :half], folded[:, half:])
-        high = folded.astype(jnp.bfloat16)
-        low = (folded - high.astype(jnp.float32)).astype(jnp.bfloat16)
-        joined = (contract(high, weight[...], ((1,), (0,)))
-                  + contract(low, weight[...], ((1,), (0,))))
-        picked = contract(pick_freq, greens[slot], ((1,), (0,)))
-        value = contract(joined, picked, ((1,), (1,)), lax.Precision.HIGHEST)
+        joined = contract(split(folded), weight[...], ((1,), (0,)))
+        joined = split(joined[:NMOM] + joined[NMOM:])
+        picked = split(contract(pick_freq, greens[slot], ((1,), (0,))))
+        value = contract(joined, picked[:LANES], ((1,), (1,)))
+        value = (value[:NMOM] + value[NMOM:]
+                 + contract(joined[:NMOM], picked[LANES:], ((1,), (1,))))
         cells_ref[...] = value if slot == OWN else cells_ref[...] + value
-
-    own_cells = NMOM * NFREQ // count
 
     def owner(i):
         to = lax.rem(me + i, count)
-        return remote(sig_send.at[to], sig_recv.at[i - 1], s_send.at[i - 1], s_recv.at[i - 1],
+        return remote(sig_send.at[to], sig_recv.at[i - 1], s_send.at[0], s_recv.at[0],
                       (to // n_pair, lax.rem(to, n_pair)))
 
     def sigma():
@@ -342,10 +371,8 @@
         cols_m = lax.broadcasted_iota(jnp.int32, (count, NMOM), 1)
         spread = jnp.zeros((count, LANES), jnp.float32)
         if own_cells >= NFREQ:
-            group = own_cells // NFREQ
-            for k in range(group):
-                pick = (cols_m == rows_d * group + k).astype(jnp.float32)
-                value = contract(pick, value_cells, ((1,), (0,)), lax.Precision.HIGHEST)
+            for k in range(folds):
+                value = value_cells[k * count:(k + 1) * count, :]
                 spread = spread + (pltpu.roll(value, NFREQ * k, 1) if k else value)
         else:
             group = NFREQ // own_cells
@@ -356,22 +383,24 @@
         factor = 1.0 / math.sqrt(5.0 * n_tiles * n_blk * states * states / (NMOM * NFREQ))
         sig_send[...] = (spread * (factor * out_scale)).reshape(count, 1, LANES)
 
-        def send_cells(i, carry):
-            owner(i).start()
-            return carry
-
-        lax.fori_loop(1, count, send_cells, 0)
-
-    share = n_tiles // 2
+        if count <= 32:
+            for i in range(1, count):
+                owner(i).start()
+        else:
+            def send_cells(i, carry):
+                owner(i).start()
+                return carry
+
+            lax.fori_loop(1, count, send_cells, 0)
 
     def compute_inner(slot, part):
         upper = greens[slot, own_rows, :]
-        for t in range(part * share, (part + 1) * share):
+        for t in (part,):
             inner[slot, pl.ds(t * half, half), :] = contract(
                 upper, tiles[t], ((1,), (0,))).astype(jnp.bfloat16)
 
     started = set()
-    pending = {(0, part): 5 for part in range(2)} | {(1, part): 7 for part in range(2)}
+    pending = {(0, part): 5 for part in range(n_tiles)} | {(1, part): 7 for part in range(n_tiles)}
 
     def compute_chi(group, slot, part, k_half=None):
         rows = own_rows if group == 0 else rest_rows
@@ -380,7 +409,7 @@
         started.add((group, part))
         pending[group, part] -= 1
         last = pending[group, part] == 0
-        for t in range(part * share, (part + 1) * share):
+        for t in (part,):
             lines = pl.ds(t * half, half)
             value = contract(inner[slot, lines, cols], greens[slot, rows, cols], ((1,), (1,)))
             if not first:
@@ -432,7 +461,7 @@
                 (to_peer(at) if kind == "p" else forward(ACROSS, at)).wait_recv()
                 waited[kind] += 1
 
-    for task in plan(total):
+    for task in plan(total, n_tiles):
         kind = task[0]
         if kind == "y":
             take_y(task[1])
@@ -462,29 +491,30 @@
         elif kind == "rest":
             compute_chi(1, task[1], task[3], None if task[1] < RELAYED else task[2])
 
-    for k in range(total):
-        exchange(k, 1 - p).wait_send()
-        to_across(k).wait_send()
-        to_peer(k).wait_send()
-        forward(ACROSS, k).wait_send()
-        if k < middle:
-            to_along(k).wait_send()
-
-            @pl.when(wrap_recv)
-            def _():
-                to_other(k).wait_send()
-        else:
-            @pl.when(jnp.logical_not(wrap_send))
-            def _():
-                to_along(k).wait_send()
+    remote(sending, arrived, y_send.at[0], y_recv.at[0], other).wait_send()
+    remote(greens.at[OWN], greens.at[ACROSS], x_send.at[0], x_recv.at[0], across).wait_send()
+    remote(greens.at[OWN], greens.at[PEER], p_send.at[0], p_recv.at[0], peer).wait_send()
+    remote(greens.at[ACROSS], greens.at[FORWARDED], f_send.at[0], f_recv.at[0], peer).wait_send()
+    upper = pl.ds(0, half)
+    remote(greens.at[ACROSS, upper], greens.at[RELAYED, upper], z_send.at[0], z_recv.at[0],
+           along).wait_send()
+
+    @pl.when(jnp.logical_not(wrap_send))
+    def _():
+        remote(greens.at[ACROSS, upper], greens.at[RELAYED, upper], z_send.at[1], z_recv.at[0],
+               along).wait_send()
+
+    @pl.when(wrap_recv)
+    def _():
+        remote(greens.at[RELAYED, upper], greens.at[RELAYED, upper], w_send.at[0], z_recv.at[0],
+               other).wait_send()
+
     send_tiles().wait_send()
     send_back().wait_send()
 
-    def take_cells(i, carry):
-        owner(i).wait()
-        return carry
-
-    lax.fori_loop(1, count, take_cells, 0)
+    cell_block = remote(sig_send.at[pl.ds(0, count - 1)], sig_recv, s_send.at[0], s_recv.at[0], peer)
+    cell_block.wait_send()
+    cell_block.wait_recv()
     summed = jnp.sum(sig_recv[...], axis=0) + sig_send[me]
     sigma_ref[...] = summed[0, :own_cells]
 
@@ -534,7 +564,8 @@
                 pltpu.VMEM((count, 1, LANES), f32),
                 pltpu.VMEM((count - 1, 1, LANES), f32),
                 dma((SPLIT + PIECES + 2,)),
-            ] + [dma((chunks,))] * 11 + [dma((2,))] * 2 + [dma((count - 1,))] * 2 + [
+            ] + [dma((1,)), dma((chunks,))] * 2 + [dma((2,)), dma((chunks,))] + [dma((1,)), dma((chunks,))] * 2 + [
+                dma((1,))] + [dma((2,))] * 2 + [dma((1,))] * 2 + [
                 pltpu.SemaphoreType.REGULAR((rounds,))],
             compiler_params=pltpu.CompilerParams(
                 collective_id=0, has_side_effects=True, vmem_limit_bytes=60 * 1024 * 1024

time: 39.6 us -> 36.9 us (0.932)
  Pallas kernels: 36.7 us -> 33.9 us
    pallas_call x1, Pallas kernels: 36.7 us -> 33.9 us  [per_device(): pl.pallas_call(lambda *refs: body(sizes, *refs), out_shape=(pltpu.VMEM((n...]
where the time goes in v3:
time: 36.9 us; the launch traced here: 36.7 us
  Pallas kernels  33.9 us (92%)
  local copies, waits for them, and re-layouts  1.48 us (4%)
  between operations  1.29 us (3%)
    pallas_call x1, Pallas kernels, per_device(): pl.pallas_call(lambda *refs: body(sizes, *refs), out_shape=(pltpu.VMEM((n...  33.9 us
    unnamed x2, local copies, waits for them, and re-layouts  1.48 us

profile of v3, /device:TPU:0, one launch (start us, length us, event | category | flops | bytes accessed | tf_op | source)
XLA Modules:
  0.0 36.7 jit_solution(9475994600416412856)
XLA Ops:
  1.3 33.9 %measure_green.1 = (bf16[4,256,512]{2,1,0:T(8,128)(2,1)S(1)}, f32[64]{0:T(128)S(1)}) custom-call(s32[1]{0:T(128)S(6)} %copy.13.refs_0_, s32[1,512]{1,0:T(1,128)} %bitcast.2, s32[1,512]{1,0:T(1,128)} %bitcast.3, bf16[1,1024,2048]{2,1,0:T(8,128)(2,1)} %refs_3_.1, bf16[1,1024,512]{2,1,0:T(8,128)(2,1)} %refs_4_.1, bf16[1,2048,512]{2,1,0:T(8,128)(2,1)} %refs_5_.1, ...), custom_call_target="tpu_custom_call" | custom-call | tf_op jit(solution)/shard_map/measure_green/pallas_call | solution.py:536
  35.2 1.0 %copy.11 = bf16[4,256,512]{2,1,0:T(8,128)(2,1)} copy(bf16[4,256,512]{2,1,0:T(8,128)(2,1)S(1)} %get-tuple-element.2) | data formatting | bytes 2097152
  36.2 0.5 %copy.12 = f32[64]{0:T(128)} copy(f32[64]{0:T(128)S(1)} %get-tuple-element.3) | data formatting | bytes 512

commit v4 on v3

--- a/solution.py
+++ b/solution.py
@@ -126,15 +126,9 @@
             pl.semaphore_signal(semaphore, inc=1, device_id=device, device_id_type=MESH)
 
     def tell_column(semaphore):
-        @pl.when(jnp.logical_not(wrap_send))
-        def _():
-            tell(semaphore, (along,))
-
-        @pl.when(jnp.logical_not(wrap_recv))
-        def _():
-            tell(semaphore, (back,))
-
-    beside = 2 - wrap_send.astype(jnp.int32) - wrap_recv.astype(jnp.int32)
+        tell(semaphore, (along, back))
+
+    beside = 2
     tell(barrier, (other, across, peer))
     tell_column(barrier)
 
@@ -152,13 +146,18 @@
         pltpu.make_async_copy(freq_hbm, freq_ref, small_sem.at[2]),
     ]
     load_left = pltpu.make_async_copy(left_hbm.at[0], left, load_sem.at[SPLIT + pieces])
-    load_tiles = pltpu.make_async_copy(tiles_hbm, tiles, load_sem.at[SPLIT + 1 + pieces])
     load_vertex = []
     for i in range(pieces):
         rows = pl.ds(i * block, block)
         load_vertex.append(
             pltpu.make_async_copy(vertex_hbm.at[0, rows], vertex.at[rows], load_sem.at[SPLIT + i]))
-    queue = list(load_vertex) + [load_right(h) for h in range(1, SPLIT)] + [load_tiles] + small[1:]
+    own_rows = pl.ds(pl.multiple_of(p * half, half), half)
+    rest_rows = pl.ds(pl.multiple_of((1 - p) * half, half), half)
+    load_tiles = [
+        pltpu.make_async_copy(tiles_hbm.at[:, rows], tiles.at[:, rows], load_sem.at[at])
+        for rows, at in ((own_rows, SPLIT + 1 + pieces), (rest_rows, SPLIT + 2 + pieces))
+    ]
+    queue = list(load_vertex) + [load_right(h) for h in range(1, SPLIT)] + load_tiles[1:] + small[1:]
 
     def pump(number):
         for copy in queue[:number]:
@@ -168,6 +167,7 @@
     small[0].start()
     load_left.start()
     load_right(0).start()
+    load_tiles[0].start()
     pump(3)
 
     scale = 1.0 / math.sqrt(breadth)
@@ -213,7 +213,7 @@
     def send_back():
         return remote(back_send, back_recv, t_send.at[1], t_recv.at[1], back)
 
-    column = max(n_blk // 4 - 2, 0)
+    column = max(n_blk // 8 - 1, 0)
     rounds = column + 2
 
     def give(r):
@@ -275,8 +275,6 @@
         cols = pl.ds(pl.multiple_of(which * half, half), half)
         turned[group] = left[:, cols].T
 
-    own_rows = pl.ds(pl.multiple_of(p * half, half), half)
-    rest_rows = pl.ds(pl.multiple_of((1 - p) * half, half), half)
     out_scale = 1.0 / math.sqrt(states)
     pair_share = forwards_across.astype(jnp.float32)
 
@@ -287,7 +285,6 @@
                 value = value + tiles[t, own_rows, :].astype(jnp.float32)
             tile_sum[...] = value
             tile_send[...] = value.astype(jnp.bfloat16)
-            send_tiles().start()
         else:
             send_tiles().wait_recv()
             mine = tile_sum[...]
@@ -305,23 +302,21 @@
     load_right(0).wait()
     pump(2)
     mask_right(0)
+    load_tiles[0].wait()
+    tile_stage(0)
     carry_half(0)
     pump(len(queue))
     pl.semaphore_wait(barrier, 3 + beside)
     send_block(0, 0)
+    send_tiles().start()
     passed = 0
     give(passed)
-    load_tiles.wait()
-    tile_stage(0)
+    load_tiles[1].wait()
     for h in range(1, SPLIT):
         load_right(h).wait()
         mask_right(h)
         carry_half(h)
         partial_block(0, h)
-    for passed in range(column):
-        take(passed)
-        give(passed + 1)
-    passed = column
     tile_stage(1)
     for group in range(1, n_pair):
         turn(group)
@@ -532,7 +527,7 @@
         bf16, f32 = jnp.bfloat16, jnp.float32
         dma = pltpu.SemaphoreType.DMA
         chunks = n_pair * SPLIT * (half // SIZE)
-        rounds = max(n_blk // 4 - 2, 0) + 2
+        rounds = max(n_blk // 8 - 1, 0) + 2
         chi, cells = pl.pallas_call(
             lambda *refs: body(sizes, *refs),
             out_shape=(
@@ -563,7 +558,7 @@
                 pltpu.VMEM((NMOM, LANES), f32),
                 pltpu.VMEM((count, 1, LANES), f32),
                 pltpu.VMEM((count - 1, 1, LANES), f32),
-                dma((SPLIT + PIECES + 2,)),
+                dma((SPLIT + PIECES + 3,)),
             ] + [dma((1,)), dma((chunks,))] * 2 + [dma((2,)), dma((chunks,))] + [dma((1,)), dma((chunks,))] * 2 + [
                 dma((1,))] + [dma((2,))] * 2 + [dma((1,))] * 2 + [
                 pltpu.SemaphoreType.REGULAR((rounds,))],

time: 36.9 us -> 36.4 us (0.986)
  Pallas kernels: 33.9 us -> 33.5 us
    pallas_call x1, Pallas kernels: 33.9 us -> 33.5 us  [per_device(): pl.pallas_call(lambda *refs: body(sizes, *refs), out_shape=(pltpu.VMEM((n...]
where the time goes in v4:
time: 36.4 us; the launch traced here: 36.3 us
  Pallas kernels  33.5 us (92%)
  local copies, waits for them, and re-layouts  1.48 us (4%)
  between operations  1.29 us (4%)
    pallas_call x1, Pallas kernels, per_device(): pl.pallas_call(lambda *refs: body(sizes, *refs), out_shape=(pltpu.VMEM((n...  33.5 us
    unnamed x2, local copies, waits for them, and re-layouts  1.48 us

profile of v4, /device:TPU:0, one launch (start us, length us, event | category | flops | bytes accessed | tf_op | source)
XLA Modules:
  0.0 36.3 jit_solution(8641405449842520194)
XLA Ops:
  1.3 33.5 %measure_green.1 = (bf16[4,256,512]{2,1,0:T(8,128)(2,1)S(1)}, f32[64]{0:T(128)S(1)}) custom-call(s32[1]{0:T(128)S(6)} %copy.13.refs_0_, s32[1,512]{1,0:T(1,128)} %bitcast.2, s32[1,512]{1,0:T(1,128)} %bitcast.3, bf16[1,1024,2048]{2,1,0:T(8,128)(2,1)} %refs_3_.1, bf16[1,1024,512]{2,1,0:T(8,128)(2,1)} %refs_4_.1, bf16[1,2048,512]{2,1,0:T(8,128)(2,1)} %refs_5_.1, ...), custom_call_target="tpu_custom_call" | custom-call | tf_op jit(solution)/shard_map/measure_green/pallas_call | solution.py:531
  34.8 1.0 %copy.11 = bf16[4,256,512]{2,1,0:T(8,128)(2,1)} copy(bf16[4,256,512]{2,1,0:T(8,128)(2,1)S(1)} %get-tuple-element.2) | data formatting | bytes 2097152
  35.8 0.5 %copy.12 = f32[64]{0:T(128)} copy(f32[64]{0:T(128)S(1)} %get-tuple-element.3) | data formatting | bytes 512

commit v5 on v4

--- a/solution.py
+++ b/solution.py
@@ -12,7 +12,7 @@
 LANES = 128
 SIZE = 128
 SPLIT = 2
-PIECES = 8
+PIECES = 4
 MESH = pl.DeviceIdType.MESH
 OWN, PEER, ACROSS, RELAYED, FORWARDED = range(5)
 
@@ -168,7 +168,7 @@
     load_left.start()
     load_right(0).start()
     load_tiles[0].start()
-    pump(3)
+    pump(2)
 
     scale = 1.0 / math.sqrt(breadth)
     per = half // SIZE
@@ -297,10 +297,10 @@
     small[0].wait()
     order = order_ref[0]
     load_left.wait()
-    pump(2)
+    pump(1)
     turn(0)
     load_right(0).wait()
-    pump(2)
+    pump(1)
     mask_right(0)
     load_tiles[0].wait()
     tile_stage(0)

time: 36.4 us -> 35.6 us (0.978)
  Pallas kernels: 33.5 us -> 32.7 us
    pallas_call x1, Pallas kernels: 33.5 us -> 32.7 us  [per_device(): pl.pallas_call(lambda *refs: body(sizes, *refs), out_shape=(pltpu.VMEM((n...]
where the time goes in v5:
time: 35.6 us; the launch traced here: 35.4 us
  Pallas kernels  32.7 us (92%)
  local copies, waits for them, and re-layouts  1.48 us (4%)
  between operations  1.29 us (4%)
    pallas_call x1, Pallas kernels, per_device(): pl.pallas_call(lambda *refs: body(sizes, *refs), out_shape=(pltpu.VMEM((n...  32.7 us
    unnamed x2, local copies, waits for them, and re-layouts  1.48 us

profile of v5, /device:TPU:0, one launch (start us, length us, event | category | flops | bytes accessed | tf_op | source)
XLA Modules:
  0.0 35.4 jit_solution(7006507749193023794)
XLA Ops:
  1.3 32.7 %measure_green.1 = (bf16[4,256,512]{2,1,0:T(8,128)(2,1)S(1)}, f32[64]{0:T(128)S(1)}) custom-call(s32[1]{0:T(128)S(6)} %copy.13.refs_0_, s32[1,512]{1,0:T(1,128)} %bitcast.2, s32[1,512]{1,0:T(1,128)} %bitcast.3, bf16[1,1024,2048]{2,1,0:T(8,128)(2,1)} %refs_3_.1, bf16[1,1024,512]{2,1,0:T(8,128)(2,1)} %refs_4_.1, bf16[1,2048,512]{2,1,0:T(8,128)(2,1)} %refs_5_.1, ...), custom_call_target="tpu_custom_call" | custom-call | tf_op jit(solution)/shard_map/measure_green/pallas_call | solution.py:531
  34.0 1.0 %copy.11 = bf16[4,256,512]{2,1,0:T(8,128)(2,1)} copy(bf16[4,256,512]{2,1,0:T(8,128)(2,1)S(1)} %get-tuple-element.2) | data formatting | bytes 2097152
  34.9 0.5 %copy.12 = f32[64]{0:T(128)} copy(f32[64]{0:T(128)S(1)} %get-tuple-element.3) | data formatting | bytes 512
